TPU v7x, 32 devices: a whole 2x2x4 slice. The times are simulated.
32 devices in a mesh: kpt: 2 (over x), grid: 16 (over z, y, core).
Axes of the slice: x: 2, y: 2, z: 4, core: 2. Of those that a mesh axis runs over, the one named last changes fastest.
Arguments:
- orbitals: bfloat16 [4, 2, 2, 512, 256, 256], P('kpt', None, None, 'grid'), may hold values from -6 to 6
- kweights: int32 [4], P('kpt'), may hold values from 1 to 16
- occupations: int32 [4, 2], P('kpt'), may hold values from 0 to 2
- z_basis: float32 [512, 512], replicated, may hold values from -0.25 to 0.25
- z_eigen: float32 [512], replicated, may hold values from 0.25 to 4
Outputs:
- potential: float32 [512, 256, 256], P('grid')
All inputs are finite; a program needn't handle non-finite values.
Results may differ from a plain program's by a relative error of at most 0.0003.
Values sent between devices are 32-bit elements; how exact they have to be, the bound alone decides.
No kernel may reach another device: no remote copies, remote signals or barrier semaphores. Data moves between devices by JAX's collectives and lax.ppermute only.
A program may use at most 128 MiB of HBM per device.

v0:
```python
from functools import partial
import jax
import jax.numpy as jnp
from jax import lax
from jax.sharding import PartitionSpec as P

precise = lax.Precision.HIGHEST


def real_basis(length):
    position = jnp.arange(length, dtype=jnp.int32)
    product = position[:, None] * position[None, :] % length
    angles = product.astype(jnp.float32) * (2.0 * jnp.pi / length)
    lower = position[:, None] <= length // 2
    table = jnp.where(lower, jnp.cos(angles), jnp.sin(angles))
    edges = (position == 0) | (position == length // 2)
    weights = jnp.where(edges, 1.0, 2.0).astype(jnp.float32) / length
    return (table, table * weights[:, None])


def forward_real(density, bases):
    table_x, scaled_x, table_y, scaled_y = bases
    along = jnp.einsum("zxy,ky->zxk", density, table_y, precision=precise)
    return jnp.einsum("jx,zxk->zjk", table_x, along, precision=precise)[None]


def inverse_real(planes, bases):
    table_x, scaled_x, table_y, scaled_y = bases
    half_done = jnp.einsum("jx,zjk->zxk", scaled_x, planes[0], precision=precise)
    return jnp.einsum("zxk,ky->zxy", half_done, scaled_y, precision=precise)


def scale_table(z_eigen, kx_start, kx_count, x_length, y_length):
    wave_x = (kx_start + jnp.arange(kx_count, dtype=jnp.int32)).astype(jnp.float32)
    wave_y = jnp.arange(y_length, dtype=jnp.int32).astype(jnp.float32)
    shift_x = 2.0 * jnp.sin(jnp.pi * wave_x / x_length)
    shift_y = 2.0 * jnp.sin(jnp.pi * wave_y / y_length)
    shifted = shift_x[:, None] ** 2 + shift_y[None, :] ** 2
    return 1.0 / (z_eigen[:, None, None] + shifted[None])


def kernel_columns(z_rows, factors, columns):
    projected = jnp.einsum("zj,czab->cjab", z_rows, columns, precision=precise)
    return jnp.einsum("zj,cjab->czab", z_rows, projected * factors[None], precision=precise)


def on_device(orbitals, kweights, occupations, z_basis, z_eigen):
    points = orbitals.shape[0]
    band_count = orbitals.shape[1]
    x_length = orbitals.shape[4]
    y_length = orbitals.shape[5]
    factor = (kweights[:, None] * occupations).astype(jnp.float32) / (16.0 * points * band_count)
    values = orbitals.astype(jnp.float32)
    partial_sum = jnp.sum(factor[:, :, None, None, None, None] * values * values, axis=(0, 1, 2))
    table_x, scaled_x = real_basis(x_length)
    table_y, scaled_y = real_basis(y_length)
    forward = partial(forward_real, bases=(table_x, scaled_x, table_y, scaled_y))
    inverse = partial(inverse_real, bases=(table_x, scaled_x, table_y, scaled_y))
    blocks = lax.axis_size("grid")
    density = lax.psum(partial_sum, "kpt")
    spectrum = forward(density)
    kx_count = x_length // blocks
    kx_start = lax.axis_index("grid") * kx_count
    factors = scale_table(z_eigen, kx_start, kx_count, x_length, y_length)
    columns = kernel_columns(
        z_basis, factors, lax.all_to_all(spectrum, "grid", split_axis=2, concat_axis=1, tiled=True)
    )
    planes = lax.all_to_all(columns, "grid", split_axis=1, concat_axis=2, tiled=True)
    potential = inverse(planes)
    return potential


def solution(mesh):
    return jax.shard_map(
        on_device,
        mesh=mesh,
        in_specs=(P("kpt", None, None, "grid", None, None), P("kpt"), P("kpt", None), P(), P()),
        out_specs=P("grid", None, None),
        check_vma=False,
    )
```

profile of v0, /device:TPU:13, one launch (start us, length us, event | category | flops | bytes accessed | tf_op | source)
XLA Modules:
  0.0 750.4 jit_solution(17960610065291599581)
XLA Ops:
  6.5 0.0 copy-start
  6.5 0.0 all-reduce.2.cloned.1.call-start
  6.5 0.8 convert_multiply_fusion
  7.4 18.9 %fusion = f32[32,256,256]{2,1,0:T(8,128)} fusion(bf16[2,2,2,32,256,256]{5,4,3,2,1,0:T(8,128)(2,1)} %param.5, f32[2,2]{1,0:T(2,128)S(1)} %convert_multiply_fusion), kind=kLoop, calls=%fused_computation.1 | loop fusion | flops 65011712 | bytes 41943056 | tf_op jit(solution)/shard_map/reduce_sum | solution.py:54
  26.3 0.0 all-reduce.2.cloned.1.call-update
  26.4 199.1 %all-reduce.2.cloned.1.call-done = f32[32,256,256]{2,1,0:T(8,128)} async-done(((f32[32,256,256]{2,1,0:T(8,128)}), f32[32,256,256]{2,1,0:T(8,128)}) %all-reduce.2.cloned.1.call-update) | async-done | bytes 8388624 | tf_op jit(solution)/shard_map/psum | solution.py:60
  225.5 12.7 %fusion.25 = f32[32,256,256]{1,2,0:T(8,128)S(1)} fusion(f32[32,256,256]{2,1,0:T(8,128)} %all-reduce.2.cloned.1.call-done, pred[256]{0:T(512)(128)(4,1)S(1)} %iota_compare_fusion), kind=kOutput, calls=%fused_computation.28 | convolution fusion | flops 6443433984 | bytes 16777472 | tf_op jit(solution)/shard_map/zxy,ky->zxk/dot_general | solution.py:23
  238.2 23.2 %convolution_bitcast_fusion = f32[1,32,256,256]{2,3,1,0:T(8,128)} fusion(f32[32,256,256]{1,2,0:T(8,128)S(1)} %fusion.25, pred[256]{0:T(512)(128)(4,1)S(1)} %iota_compare_fusion), kind=kOutput, calls=%fused_computation.14 | convolution fusion | flops 6443433984 | bytes 16777472 | tf_op jit(solution)/shard_map/jx,zxk->zjk/dot_general | solution.py:24
  261.4 10.3 %copy.13 = f32[1,32,256,256]{3,1,0,2:T(8,128)} copy(f32[1,32,256,256]{2,3,1,0:T(8,128)} %convolution_bitcast_fusion) | data formatting | bytes 16777216 | tf_op jit(solution)/shard_map/broadcast_in_dim | solution.py:24
  271.7 6.5 all-to-all-start
  278.3 0.1 broadcast_add_fusion
  278.4 182.2 %all-to-all-done = f32[1,32,256,256]{3,1,0,2:T(8,128)} async-done(((f32[1,32,256,256]{3,1,0,2:T(8,128)}), f32[1,32,256,256]{3,1,0,2:T(8,128)}, u32[]{:S(2)}, u32[]{:S(2)}) %all-to-all-start) | async-done | bytes 8388640 | tf_op jit(solution)/shard_map/all_to_all | solution.py:66
  460.6 8.2 %copy.14 = f32[1,32,256,256]{3,2,1,0:T(8,128)S(1)} copy(f32[1,32,256,256]{3,1,0,2:T(8,128)} %all-to-all-done) | data formatting | bytes 16777216 | tf_op jit(solution)/shard_map/all_to_all | solution.py:66
  468.8 1.4 copy.15
  470.2 0.0 copy-done
  470.2 0.0 copy-start.2
  470.2 21.4 %fusion.6 = f32[16,256,512]{2,1,0:T(8,128)S(1)} fusion(f32[512,16,256]{2,1,0:T(8,128)S(1)} %bitcast.51, f32[512,512]{1,0:T(8,128)S(1)} %copy-done), kind=kOutput, calls=%fused_computation.7 | convolution fusion | flops 12884901888 | bytes 17825792 | tf_op jit(solution)/shard_map/zj,czab->cjab/dot_general | solution.py:43
  491.7 0.0 copy-done.2
  491.7 16.4 %fusion.13 = f32[1,512,16,256]{1,3,2,0:T(8,128)} fusion(f32[16,256,512]{2,1,0:T(8,128)S(1)} %fusion.6, f32[16,256]{1,0:T(8,128)S(1)} %broadcast_add_fusion, f32[512]{0:T(512)S(1)} %copy-done.2, f32[512,512]{1,0:T(8,128)S(1)} %copy-done), kind=kOutput, calls=%fused_computation.15 | convolution fusion | flops 12891193344 | bytes 17844224 | tf_op jit(solution)/shard_map/zj,cjab->czab/dot_general | solution.py:44
  508.1 10.3 %copy.17 = f32[1,512,16,256]{3,2,0,1:T(8,128)} copy(f32[1,512,16,256]{1,3,2,0:T(8,128)} %fusion.13) | data formatting | bytes 16777216 | tf_op jit(solution)/shard_map/zj,cjab->czab/transpose | solution.py:44
  518.3 5.0 all-to-all-start.1
  523.3 182.1 %all-to-all-done.1 = f32[1,512,16,256]{3,2,0,1:T(8,128)} async-done(((f32[1,512,16,256]{3,2,0,1:T(8,128)}), f32[1,512,16,256]{3,2,0,1:T(8,128)}, u32[]{:S(2)}, u32[]{:S(2)}) %all-to-all-start.1) | async-done | bytes 8388640 | tf_op jit(solution)/shard_map/all_to_all | solution.py:68
  705.5 4.4 copy.18
  709.8 0.0 copy-start.1
  709.8 15.4 %fusion.22 = f32[32,256,256]{2,1,0:T(8,128)S(1)} fusion(f32[32,256,256]{2,1,0:T(8,128)S(1)} %bitcast.52, f32[256]{0:T(256)S(1)} %fusion.34, pred[256]{0:T(512)(128)(4,1)S(1)} %iota_compare_fusion), kind=kOutput, calls=%fused_computation.25 | convolution fusion | flops 6443499520 | bytes 16778496 | tf_op jit(solution)/shard_map/jx,zjk->zxk/dot_general | solution.py:29
  725.3 17.9 %fusion.4 = f32[32,256,256]{2,1,0:T(8,128)} fusion(f32[32,256,256]{2,1,0:T(8,128)S(1)} %fusion.22, f32[256]{0:T(256)S(1)} %fusion.34, pred[256]{0:T(512)(128)(4,1)S(1)} %iota_compare_fusion), kind=kOutput, calls=%fused_computation.5 | convolution fusion | flops 6443499520 | bytes 16778496 | tf_op jit(solution)/shard_map/zxk,ky->zxy/dot_general | solution.py:30
  743.2 0.0 copy-done.1
  (4 shorter events, 0.1 us)
Async XLA Ops:
  6.5 463.7 %copy-start = (f32[512,512]{1,0:T(8,128)S(1)}, f32[512,512]{1,0:T(8,128)}, u32[]{:S(2)}) copy-start(f32[512,512]{1,0:T(8,128)} %param.8) | copy-start | bytes 3145732
  6.5 219.0 %all-reduce.2.cloned.1.call-start = ((), (), s32[]{:S(2)}) async-start(), calls=%async_computation.2 | async-start | bytes 16777216 | tf_op jit(solution)/shard_map/psum | solution.py:60
  271.7 188.9 %all-to-all-start = ((f32[1,32,256,256]{3,1,0,2:T(8,128)}), f32[1,32,256,256]{3,1,0,2:T(8,128)}, u32[]{:S(2)}, u32[]{:S(2)}) async-start(f32[1,32,256,256]{3,1,0,2:T(8,128)} %copy.13), calls=%async_computation | async-start | bytes 16777216 | tf_op jit(solution)/shard_map/all_to_all | solution.py:66
  470.2 21.4 %copy-start.2 = (f32[512]{0:T(512)S(1)}, f32[512]{0:T(512)}, u32[]{:S(2)}) copy-start(f32[512]{0:T(512)} %param.9) | copy-start | bytes 6148
  518.3 187.1 %all-to-all-start.1 = ((f32[1,512,16,256]{3,2,0,1:T(8,128)}), f32[1,512,16,256]{3,2,0,1:T(8,128)}, u32[]{:S(2)}, u32[]{:S(2)}) async-start(f32[1,512,16,256]{3,2,0,1:T(8,128)} %copy.17), calls=%async_computation.1 | async-start | bytes 16777216 | tf_op jit(solution)/shard_map/all_to_all | solution.py:68
  709.8 33.3 %copy-start.1 = (f32[512,512]{1,0:T(8,128)S(1)}, f32[512,512]{1,0:T(8,128)}, u32[]{:S(2)}) copy-start(f32[512,512]{1,0:T(8,128)} %param.8) | copy-start | bytes 3145732
Sparse Core Ops, SparseCore 0:
  26.5 198.9 all-reduce.1
where the time goes:
time: 759 us; the launch traced here: 750 us
  waiting for transfers between devices  563 us (74%)
  matrix products  107 us (14%)
  local copies, waits for them, and re-layouts  34.6 us (5%)
  other arithmetic  20 us (3%)
  between operations  13.9 us (2%)
  starting transfers between devices  11.5 us (2%)
    psum x1, waiting for transfers between devices, on_device(): density = lax.psum(partial_sum, 'kpt')  199 us
    all_to_all x1, waiting for transfers between devices, on_device(): lax.all_to_all(spectrum, 'grid', split_axis=2, concat_axis=1, tiled=True)  182 us
    all_to_all x1, waiting for transfers between devices, on_device(): lax.all_to_all(columns, 'grid', split_axis=1, concat_axis=2, tiled=True)  182 us
    dot_general x1, matrix products, forward_real(): return jnp.einsum('jx,zxk->zjk', table_x, along, precision=precise)[None]  23.2 us
    dot_general x1, matrix products, kernel_columns(): projected = jnp.einsum('zj,czab->cjab', z_rows, columns, precision=precise)  21.4 us
    reduce_sum x1, other arithmetic, on_device(): jnp.sum(factor[:, :, None, None, None, None] * values * values, axis=(0,...  18.9 us
    dot_general x1, matrix products, inverse_real(): return jnp.einsum('zxk,ky->zxy', half_done, scaled_y, precision=precise)  17.9 us
    dot_general x1, matrix products, kernel_columns(): jnp.einsum('zj,cjab->czab', z_rows, projected * factors[None], precision=...  16.4 us
  transfers between devices with their start and end apart: 3, of which 3 were waited for; matrix products, arithmetic and copies ran while one was open for 0% of the time, Pallas kernels for 0%

commit v1 on v0

--- a/solution.py
+++ b/solution.py
@@ -63,7 +63,14 @@
     kx_start = lax.axis_index("grid") * kx_count
     factors = scale_table(z_eigen, kx_start, kx_count, x_length, y_length)
     columns = kernel_columns(
-        z_basis, factors, lax.all_to_all(spectrum, "grid", split_axis=2, concat_axis=1, tiled=True)
+        z_basis,
+        factors,
+        jnp.concatenate(
+            lax.all_to_all(
+                jnp.stack(jnp.split(spectrum, lax.axis_size("grid"), axis=2)), "grid", 0, 0
+            ),
+            axis=1,
+        ),
     )
     planes = lax.all_to_all(columns, "grid", split_axis=1, concat_axis=2, tiled=True)
     potential = inverse(planes)

time: 759 us -> 731 us (0.963)
  matrix products: 107 us -> 88.9 us
    dot_general x1, matrix products: 23.2 us -> 10.1 us  [forward_real(): return jnp.einsum('jx,zxk->zjk', table_x, along, precision=precise)[None]]
    unnamed x6 -> x21, local copies, waits for them, and re-layouts: 0.02 us -> 12.6 us
    broadcast_in_dim x1 -> x0, local copies, waits for them, and re-layouts: 10.3 us -> none  [forward_real(): return jnp.einsum('jx,zxk->zjk', table_x, along, precision=precise)[None]]
    all_to_all x2 -> x0, local copies, waits for them, and re-layouts: 9.66 us -> none  [on_device(): lax.all_to_all(spectrum, 'grid', split_axis=2, concat_axis=1, tiled=True)]
where the time goes in v1:
time: 731 us; the launch traced here: 726 us
  waiting for transfers between devices  563 us (77%)
  matrix products  88.9 us (12%)
  local copies, waits for them, and re-layouts  28.1 us (4%)
  other arithmetic  20 us (3%)
  between operations  13.7 us (2%)
  starting transfers between devices  12 us (2%)
    psum x1, waiting for transfers between devices, on_device(): density = lax.psum(partial_sum, 'kpt')  199 us
    all_to_all x1, waiting for transfers between devices, on_device(): lax.all_to_all(jnp.stack(jnp.split(spectrum, lax.axis_size('grid'), axis=...  182 us
    all_to_all x1, waiting for transfers between devices, on_device(): lax.all_to_all(columns, 'grid', split_axis=1, concat_axis=2, tiled=True)  182 us
    reduce_sum x1, other arithmetic, on_device(): jnp.sum(factor[:, :, None, None, None, None] * values * values, axis=(0,...  18.9 us
    dot_general x1, matrix products, inverse_real(): return jnp.einsum('zxk,ky->zxy', half_done, scaled_y, precision=precise)  17.9 us
    dot_general x1, matrix products, kernel_columns(): projected = jnp.einsum('zj,czab->cjab', z_rows, columns, precision=precise)  17.3 us
    dot_general x1, matrix products, kernel_columns(): jnp.einsum('zj,cjab->czab', z_rows, projected * factors[None], precision=...  16.4 us
    dot_general x1, matrix products, inverse_real(): jnp.einsum('jx,zjk->zxk', scaled_x, planes[0], precision=precise)  15.4 us
  transfers between devices with their start and end apart: 3, of which 3 were waited for; matrix products, arithmetic and copies ran while one was open for 0% of the time, Pallas kernels for 0%

profile of v1, /device:TPU:13, one launch (start us, length us, event | category | flops | bytes accessed | tf_op | source)
XLA Modules:
  0.0 725.9 jit_solution(302729634033786531)
XLA Ops:
  6.5 0.8 convert_multiply_fusion
  7.4 18.9 %fusion = f32[32,256,256]{2,1,0:T(8,128)} fusion(bf16[2,2,2,32,256,256]{5,4,3,2,1,0:T(8,128)(2,1)} %param.5, f32[2,2]{1,0:T(2,128)S(1)} %convert_multiply_fusion), kind=kLoop, calls=%fused_computation.1 | loop fusion | flops 65011712 | bytes 41943056 | tf_op jit(solution)/shard_map/reduce_sum | solution.py:54
  26.4 199.1 %all-reduce.2.cloned.1.call-done = f32[32,256,256]{2,1,0:T(8,128)} async-done(((f32[32,256,256]{2,1,0:T(8,128)}), f32[32,256,256]{2,1,0:T(8,128)}) %all-reduce.2.cloned.1.call-update) | async-done | bytes 8388624 | tf_op jit(solution)/shard_map/psum | solution.py:60
  225.5 11.9 %fusion.41 = f32[32,256,256]{2,1,0:T(8,128)S(1)} fusion(f32[32,256,256]{2,1,0:T(8,128)} %all-reduce.2.cloned.1.call-done, pred[256]{0:T(512)(128)(4,1)S(1)} %iota_compare_fusion), kind=kOutput, calls=%fused_computation.60 | convolution fusion | flops 6443433984 | bytes 16777472 | tf_op jit(solution)/shard_map/zxy,ky->zxk/dot_general | solution.py:23
  237.4 10.1 %convolution_bitcast_fusion = f32[1,32,256,256]{3,2,1,0:T(8,128)S(1)} fusion(f32[32,256,256]{2,1,0:T(8,128)S(1)} %fusion.41, pred[256]{0:T(512)(128)(4,1)S(1)} %iota_compare_fusion), kind=kOutput, calls=%fused_computation.14 | convolution fusion | flops 6443433984 | bytes 16777472 | tf_op jit(solution)/shard_map/jx,zxk->zjk/dot_general | solution.py:24
  247.5 0.8 fusion.33
  248.4 0.8 fusion.32
  249.2 0.8 fusion.31
  250.0 0.8 fusion.30
  250.9 0.8 fusion.29
  251.7 0.8 fusion.28
  252.6 0.8 fusion.27
  253.4 0.8 fusion.26
  254.2 0.8 fusion.25
  255.1 0.8 fusion.24
  255.9 0.8 fusion.23
  256.8 0.8 fusion.22
  257.6 0.8 fusion.21
  258.4 0.8 fusion.20
  259.3 0.8 fusion.19
  260.1 0.8 fusion.18
  261.0 6.9 all-to-all-start
  267.9 0.1 broadcast_add_fusion
  268.0 182.0 %all-to-all-done = f32[16,1,32,16,256]{4,3,2,1,0:T(8,128)} async-done(((f32[16,1,32,16,256]{4,3,2,1,0:T(8,128)}), f32[16,1,32,16,256]{4,3,2,1,0:T(8,128)}, u32[]{:S(2)}, u32[]{:S(2)}) %all-to-all-start) | async-done | bytes 8388640 | tf_op jit(solution)/shard_map/all_to_all | solution.py:69
  450.0 17.3 %fusion.6 = f32[16,256,512]{2,1,0:T(8,128)S(1)} fusion(f32[512,16,256]{2,1,0:T(8,128)} %bitcast.20, f32[512,512]{1,0:T(8,128)S(1)} %copy-done), kind=kOutput, calls=%fused_computation.7 | convolution fusion | flops 12884901888 | bytes 17825792 | tf_op jit(solution)/shard_map/zj,czab->cjab/dot_general | solution.py:43
  467.4 16.4 %fusion.13 = f32[1,512,16,256]{1,3,2,0:T(8,128)} fusion(f32[16,256,512]{2,1,0:T(8,128)S(1)} %fusion.6, f32[16,256]{1,0:T(8,128)S(1)} %broadcast_add_fusion, f32[512]{0:T(512)S(1)} %copy-done.2, f32[512,512]{1,0:T(8,128)S(1)} %copy-done), kind=kOutput, calls=%fused_computation.15 | convolution fusion | flops 12891193344 | bytes 17844224 | tf_op jit(solution)/shard_map/zj,cjab->czab/dot_general | solution.py:44
  483.8 10.3 %copy.11 = f32[1,512,16,256]{3,2,0,1:T(8,128)} copy(f32[1,512,16,256]{1,3,2,0:T(8,128)} %fusion.13) | data formatting | bytes 16777216 | tf_op jit(solution)/shard_map/zj,cjab->czab/transpose | solution.py:44
  494.0 5.2 all-to-all-start.1
  499.2 181.9 %all-to-all-done.1 = f32[1,512,16,256]{3,2,0,1:T(8,128)} async-done(((f32[1,512,16,256]{3,2,0,1:T(8,128)}), f32[1,512,16,256]{3,2,0,1:T(8,128)}, u32[]{:S(2)}, u32[]{:S(2)}) %all-to-all-start.1) | async-done | bytes 8388640 | tf_op jit(solution)/shard_map/all_to_all | solution.py:75
  681.2 4.4 copy.12
  685.6 15.4 %fusion.38 = f32[32,256,256]{2,1,0:T(8,128)S(1)} fusion(f32[32,256,256]{2,1,0:T(8,128)S(1)} %bitcast.112, f32[256]{0:T(256)S(1)} %fusion.50, pred[256]{0:T(512)(128)(4,1)S(1)} %iota_compare_fusion), kind=kOutput, calls=%fused_computation.57 | convolution fusion | flops 6443499520 | bytes 16778496 | tf_op jit(solution)/shard_map/jx,zjk->zxk/dot_general | solution.py:29
  700.9 17.9 %fusion.4 = f32[32,256,256]{2,1,0:T(8,128)} fusion(f32[32,256,256]{2,1,0:T(8,128)S(1)} %fusion.38, f32[256]{0:T(256)S(1)} %fusion.50, pred[256]{0:T(512)(128)(4,1)S(1)} %iota_compare_fusion), kind=kOutput, calls=%fused_computation.5 | convolution fusion | flops 6443499520 | bytes 16778496 | tf_op jit(solution)/shard_map/zxk,ky->zxy/dot_general | solution.py:30
  (12 shorter events, 0.1 us)
Async XLA Ops:
  6.5 443.5 %copy-start = (f32[512,512]{1,0:T(8,128)S(1)}, f32[512,512]{1,0:T(8,128)}, u32[]{:S(2)}) copy-start(f32[512,512]{1,0:T(8,128)} %param.8) | copy-start | bytes 3145732
  6.5 219.0 %all-reduce.2.cloned.1.call-start = ((), (), s32[]{:S(2)}) async-start(), calls=%async_computation.2 | async-start | bytes 16777216 | tf_op jit(solution)/shard_map/psum | solution.py:60
  261.0 189.1 %all-to-all-start = ((f32[16,1,32,16,256]{4,3,2,1,0:T(8,128)}), f32[16,1,32,16,256]{4,3,2,1,0:T(8,128)}, u32[]{:S(2)}, u32[]{:S(2)}) async-start(f32[16,1,32,16,256]{4,3,2,1,0:T(8,128)} %fusion.18), calls=%async_computation | async-start | bytes 16777216 | tf_op jit(solution)/shard_map/all_to_all | solution.py:69
  450.0 17.4 %copy-start.2 = (f32[512]{0:T(512)S(1)}, f32[512]{0:T(512)}, u32[]{:S(2)}) copy-start(f32[512]{0:T(512)} %param.9) | copy-start | bytes 6148
  494.0 187.2 %all-to-all-start.1 = ((f32[1,512,16,256]{3,2,0,1:T(8,128)}), f32[1,512,16,256]{3,2,0,1:T(8,128)}, u32[]{:S(2)}, u32[]{:S(2)}) async-start(f32[1,512,16,256]{3,2,0,1:T(8,128)} %copy.11), calls=%async_computation.1 | async-start | bytes 16777216 | tf_op jit(solution)/shard_map/all_to_all | solution.py:75
  685.6 33.2 %copy-start.1 = (f32[512,512]{1,0:T(8,128)S(1)}, f32[512,512]{1,0:T(8,128)}, u32[]{:S(2)}) copy-start(f32[512,512]{1,0:T(8,128)} %param.8) | copy-start | bytes 3145732
Sparse Core Ops, SparseCore 0:
  26.5 198.9 all-reduce.1
